TPU v7x, 32 devices: a whole 2x2x4 slice. The times are simulated.
32 devices in a mesh: tm: 8 (over y, x, core), cell: 4 (over z).
Axes of the slice: x: 2, y: 2, z: 4, core: 2. Of those that a mesh axis runs over, the one named last changes fastest.
Arguments:
- anomalies: bfloat16 [24, 2, 8192, 256], P('tm', None, 'cell'), may hold values from -6 to 6
- obs_cells: int32 [24, 128], P('tm', 'cell'), may hold values from 0 to 8191, as said below
- obs_counts: int32 [24, 4], P('tm', 'cell'), may hold values from 16 to 32
- obs_precision: float32 [24, 128], P('tm', 'cell'), may hold values from 0.1 to 1
- inflation: float32 [24], P('tm'), may hold values from 1 to 1.12
Outputs:
- smoothed: bfloat16 [24, 2, 8192, 256], P('tm', None, 'cell')
Inputs may be any that keep to these rules, and one draw needn't show every extreme that they name: `obs_cells`: slot k of a window names a cell of the block of 2048 cells that starts at (k // 32) * 2048; two slots may name the same cell.
All inputs are finite; a program needn't handle non-finite values.
Results may differ from a plain program's by a relative error of at most 0.017.
Values may be sent and summed in bfloat16 or wider, within the bound.
A program may use at most 128 MiB of HBM per device.

v0:
```python
import jax
import jax.numpy as jnp
from jax import lax
from jax.experimental import pallas as pl
from jax.experimental.pallas import tpu as pltpu
from jax.sharding import PartitionSpec as P

F32 = jnp.float32
BF16 = jnp.bfloat16


def dot_any(left, right, dims):
    return lax.dot_general(left, right, (dims, ((), ())), preferred_element_type=F32)


def halves(value):
    high = value.astype(BF16)
    return high, (value - high.astype(F32)).astype(BF16)


def dot_three(left, right, dims=((1,), (0,))):
    lh, ll = halves(left)
    rh, rl = halves(right)
    return dot_any(lh, rh, dims) + (dot_any(lh, rl, dims) + dot_any(ll, rh, dims))


def dot_full(left, right, dims=((1,), (0,))):
    return lax.dot_general(
        left, right, (dims, ((), ())), precision=lax.Precision.HIGHEST, preferred_element_type=F32
    )


def eliminate(matrices):
    size = matrices[0].shape[0]
    groups = size // 8
    lane = lax.broadcasted_iota(jnp.int32, (8, size), 1)
    sub = lax.broadcasted_iota(jnp.int32, (8, size), 0)
    work = [[m[8 * g : 8 * g + 8, :] for g in range(groups)] for m in matrices]
    for k in range(0, size, 2):
        g, r = divmod(k, 8)
        first_lane, second_lane = lane == k, lane == k + 1
        either = first_lane | second_lane
        for rows in work:
            own = rows[g]
            near = jnp.broadcast_to(own[:, k : k + 1], (8, size))
            far = jnp.broadcast_to(own[:, k + 1 : k + 2], (8, size))
            d0 = jnp.broadcast_to(near[r : r + 1, :], (8, size))
            m = jnp.broadcast_to(near[r + 1 : r + 2, :], (8, size))
            e = jnp.broadcast_to(far[r + 1 : r + 2, :], (8, size))
            row0 = jnp.broadcast_to(own[r : r + 1, :], (8, size))
            row1 = jnp.broadcast_to(own[r + 1 : r + 2, :], (8, size))
            i0 = 1.0 / d0
            step = m * i0
            i1 = 1.0 / (e - step * m)
            row0_one = jnp.where(first_lane, 1.0, row0)
            row1_mid = jnp.where(first_lane, 0.0, row1) - step * row0_one
            p0 = jnp.where(second_lane, 0.0, row0_one) * i0
            p1 = jnp.where(second_lane, 1.0, row1_mid) * i1
            for i in range(g, groups):
                if i == g:
                    c0, c1 = near, far
                else:
                    c0 = jnp.broadcast_to(rows[i][:, k : k + 1], (8, size))
                    c1 = jnp.broadcast_to(rows[i][:, k + 1 : k + 2], (8, size))
                c1 = c1 - c0 * step
                new = jnp.where(either, 0.0, rows[i]) - c0 * p0 - c1 * p1
                if i == g:
                    new = jnp.where(sub <= r, own, jnp.where(sub == r + 1, row1_mid, new))
                rows[i] = new
    results = []
    for rows in work:
        pieces = []
        for g in range(groups):
            row = sub + 8 * g
            pivot = jnp.sum(jnp.where(lane == row, rows[g], 0.0), axis=1, keepdims=True)
            unit = jnp.where(lane < row, rows[g], jnp.where(lane == row, 1.0, 0.0))
            pieces.append(unit * lax.rsqrt(pivot))
        results.append(jnp.concatenate(pieces, axis=0))
    return results


def transforms_kernel(
    rho_ref, picked_ref, weight_ref, partial_ref, own_ref, gram, first_inv, second_inv, low_ref, mid_ref
):
    blocks, windows, slots, members = picked_ref.shape
    half = members // 2
    slot_eye = (
        lax.broadcasted_iota(jnp.int32, (slots, slots), 0)
        == lax.broadcasted_iota(jnp.int32, (slots, slots), 1)
    )
    eye = (
        lax.broadcasted_iota(jnp.int32, (members, members), 0)
        == lax.broadcasted_iota(jnp.int32, (members, members), 1)
    )
    tn = ((0,), (0,))
    nt = ((1,), (1,))

    @pl.loop(0, windows)
    def _(w):
        rows = jnp.concatenate([picked_ref[n, w] for n in range(blocks)], axis=0)
        columns = [
            jnp.sum(
                jnp.where(slot_eye, weight_ref[n, pl.ds(w, 1), :], 0.0), axis=1, keepdims=True
            )
            for n in range(blocks)
        ]
        high, low = halves(rows.astype(F32) * jnp.concatenate(columns, axis=0))
        total = dot_any(high, rows, tn) + dot_any(low, rows, tn)
        gram[w] = total + jnp.where(eye, F32(members - 1.0), 0.0)

    for w, value in enumerate(eliminate([gram[w, :half, :half] for w in range(windows)])):
        first_inv[w] = value

    @pl.loop(0, windows)
    def _(w):
        lower = dot_full(gram[w, half:, :half], first_inv[w], nt)
        low_ref[w] = lower
        gram[w, half:, half:] -= dot_full(lower, lower, nt)
        mid_ref[w] = dot_full(lower, first_inv[w])

    for w, value in enumerate(eliminate([gram[w, half:, half:] for w in range(windows)])):
        second_inv[w] = value

    zero = jnp.zeros((half, half), F32)

    @pl.loop(0, windows)
    def _(w):
        scale = rho_ref[w] * jnp.sqrt(F32(members - 1.0))
        cross = -dot_full(second_inv[w], mid_ref[w])
        partial_ref[w, :half, :half] = scale * first_inv[w].T
        partial_ref[w, :half, half:] = scale * cross.T
        partial_ref[w, half:, :half] = zero
        partial_ref[w, half:, half:] = scale * second_inv[w].T

    @pl.loop(0, windows - 1)
    def _(turn):
        w = windows - 2 - turn
        partial_ref[w] = dot_three(partial_ref[w], partial_ref[w + 1])

    own_ref[0] = partial_ref[0, :half, :half].astype(BF16)
    own_ref[1] = partial_ref[0, :half, half:].astype(BF16)
    own_ref[2] = partial_ref[0, half:, half:].astype(BF16)


def fold_kernel(position_ref, products_ref, partial_ref, out_ref, whole, later):
    count = products_ref.shape[0]
    windows, members, _ = partial_ref.shape
    half = members // 2
    position = position_ref[0]
    whole[...] = jnp.zeros_like(whole)
    later[...] = (
        lax.broadcasted_iota(jnp.int32, (members, members), 0)
        == lax.broadcasted_iota(jnp.int32, (members, members), 1)
    ).astype(F32)

    @pl.loop(0, count - 1 - position)
    def _(turn):
        source = count - 1 - turn
        whole[:half, :half] = products_ref[source, 0]
        whole[:half, half:] = products_ref[source, 1]
        whole[half:, half:] = products_ref[source, 2]
        high, low = halves(later[...])
        left = whole[...]
        later[...] = dot_any(left, high, ((1,), (0,))) + dot_any(left, low, ((1,), (0,)))

    @pl.loop(0, windows)
    def _(w):
        out_ref[w] = dot_three(partial_ref[w], later[...]).astype(BF16)


def exchange_kernel(axis, count, one_way, items, *refs):
    ins, outs = refs[:items], refs[items : 2 * items]
    send_sem, recv_sem = refs[2 * items :]
    me = lax.axis_index(axis)
    barrier = pltpu.get_barrier_semaphore()
    for shift in range(1, count):
        pl.semaphore_signal(
            barrier,
            inc=1,
            device_id={axis: lax.rem(me + shift, count)},
            device_id_type=pl.DeviceIdType.MESH,
        )
    pl.semaphore_wait(barrier, count - 1)

    def copy_of(shift, item):
        return pltpu.make_async_remote_copy(
            src_ref=ins[item],
            dst_ref=outs[item].at[me],
            send_sem=send_sem.at[item, shift],
            recv_sem=recv_sem.at[item, shift],
            device_id={axis: lax.rem(me + count - shift, count)},
            device_id_type=pl.DeviceIdType.MESH,
        )

    def when(condition, action):
        if one_way:
            pl.when(condition)(action)
        else:
            action()

    order = [(shift, item) for shift in range(1, count) for item in range(items)]
    for shift, item in order:
        when(me >= shift, lambda: copy_of(shift, item).start())
    if not one_way:
        for item in range(items):
            outs[item][me] = ins[item][...]
    for shift, item in order:
        when(me >= shift, lambda: copy_of(shift, item).wait_send())
        when(me + shift < count, lambda: copy_of(shift, item).wait_recv())


def exchange(axis, one_way, collective_id, *values):
    count = lax.axis_size(axis)
    items = len(values)
    vmem = pl.BlockSpec(memory_space=pltpu.VMEM)
    return pl.pallas_call(
        lambda *refs: exchange_kernel(axis, count, one_way, items, *refs),
        out_shape=tuple(jax.ShapeDtypeStruct((count,) + v.shape, v.dtype) for v in values),
        in_specs=[vmem] * items,
        out_specs=(vmem,) * items,
        scratch_shapes=[
            pltpu.SemaphoreType.DMA((items, count)),
            pltpu.SemaphoreType.DMA((items, count)),
        ],
        compiler_params=pltpu.CompilerParams(collective_id=collective_id, has_side_effects=True),
        name="exchange_" + axis,
    )(*values)


def apply_kernel(field_ref, weight_ref, out_ref):
    out_ref[0] = jnp.dot(field_ref[0], weight_ref[0], preferred_element_type=F32).astype(
        out_ref.dtype
    )


def local(anomalies, obs_cells, obs_counts, obs_precision, inflation):
    windows, _, cell_width, members = anomalies.shape
    half = members // 2
    slots = obs_cells.shape[1]
    first_cell = lax.axis_index("cell") * cell_width
    offsets = obs_cells - first_cell
    picked = jax.vmap(lambda field, where_at: field[0][where_at])(anomalies, offsets)
    live = jnp.arange(slots, dtype=jnp.int32)[None, :] < obs_counts
    weights = jnp.where(live, obs_precision, jnp.float32(0.0))
    gathered, gathered_weights = exchange("cell", False, 0, picked, weights)
    vmem = pl.BlockSpec(memory_space=pltpu.VMEM)
    smem = pl.BlockSpec(memory_space=pltpu.SMEM)
    partial, own = pl.pallas_call(
        transforms_kernel,
        out_shape=(
            jax.ShapeDtypeStruct((windows, members, members), F32),
            jax.ShapeDtypeStruct((3, half, half), BF16),
        ),
        in_specs=[smem, vmem, vmem],
        out_specs=(vmem, vmem),
        scratch_shapes=[pltpu.VMEM((windows, members, members), F32)]
        + [pltpu.VMEM((windows, half, half), F32)] * 4,
        name="transforms",
    )(inflation, gathered, gathered_weights)
    (products,) = exchange("tm", True, 1, own)
    weight_mats = pl.pallas_call(
        fold_kernel,
        out_shape=jax.ShapeDtypeStruct((windows, members, members), BF16),
        in_specs=[smem, vmem, vmem],
        out_specs=vmem,
        scratch_shapes=[pltpu.VMEM((members, members), BF16), pltpu.VMEM((members, members), F32)],
        name="fold",
    )(lax.axis_index("tm").astype(jnp.int32)[None], products, partial)
    flat = anomalies.reshape(windows, 2 * cell_width, members)
    tile = min(2048, 2 * cell_width)
    result = pl.pallas_call(
        apply_kernel,
        out_shape=jax.ShapeDtypeStruct(flat.shape, BF16),
        grid=(windows, 2 * cell_width // tile),
        in_specs=[
            pl.BlockSpec((1, tile, members), lambda w, c: (w, c, 0)),
            pl.BlockSpec((1, members, members), lambda w, c: (w, 0, 0)),
        ],
        out_specs=pl.BlockSpec((1, tile, members), lambda w, c: (w, c, 0)),
        name="apply",
    )(flat, weight_mats)
    return result.reshape(anomalies.shape)


def solution(mesh):
    placed = (
        P("tm", None, "cell", None),
        P("tm", "cell"),
        P("tm", "cell"),
        P("tm", "cell"),
        P("tm"),
    )
    return jax.shard_map(
        local, mesh=mesh, in_specs=placed, out_specs=P("tm", None, "cell", None), check_vma=False
    )
```

profile of v0, /device:TPU:0, one launch (start us, length us, event | category | flops | bytes accessed | tf_op | source)
XLA Modules:
  0.0 71.5 jit_solution(10637145085186539722)
XLA Ops:
  0.0 0.7 fusion.3
  0.7 0.1 reshape.8
  0.8 1.3 %fusion.4.refs_1_ = f32[3,32]{1,0:T(4,128)} fusion(f32[3,32]{1,0:T(4,128)} %param.8, s32[3]{0:T(128)} %bitcast.17), kind=kLoop, calls=%fused_computation.8 | loop fusion | flops 192 | bytes 780 | tf_op jit(solution)/shard_map/jit(_where)/select_n | solution.py:244
  2.1 2.1 %slice_bitcast_fusion = bf16[3,2048,256]{2,1,0:T(8,128)(2,1)S(1)} fusion(bf16[3,2,2048,256]{3,2,1,0:T(8,128)(2,1)} %param.5), kind=kLoop, calls=%fused_computation.1 | loop fusion | bytes 6291456 | tf_op jit(solution)/shard_map/vmap()/squeeze | solution.py:242
  4.2 2.2 %gather_fusion = bf16[96,256]{1,0:T(8,128)(2,1)} fusion(bf16[3,2048,256]{2,1,0:T(8,128)(2,1)S(1)} %slice_bitcast_fusion, s32[96]{0:T(128)S(1)} %reshape.8), kind=kCustom, calls=%fused_computation | custom fusion | bytes 99072 | tf_op jit(solution)/shard_map/vmap()/gather | solution.py:242
  6.4 12.0 %exchange_cell.1 = (bf16[4,3,32,256]{3,2,1,0:T(8,128)(2,1)}, f32[4,3,32]{2,1,0:T(4,128)}) custom-call(bf16[3,32,256]{2,1,0:T(8,128)(2,1)} %bitcast.16, f32[3,32]{1,0:T(4,128)} %fusion.4.refs_1_), custom_call_target="tpu_custom_call" | custom-call | tf_op jit(solution)/shard_map/exchange_cell/pallas_call | solution.py:216
  18.4 26.1 %transforms.1 = (f32[3,256,256]{2,1,0:T(8,128)}, bf16[3,128,128]{2,1,0:T(8,128)(2,1)}) custom-call(f32[3]{0:T(128)} %rho_ref.1, bf16[4,3,32,256]{3,2,1,0:T(8,128)(2,1)} %get-tuple-element.9.picked_ref, f32[4,3,32]{2,1,0:T(4,128)} %get-tuple-element.10.weight_ref), custom_call_target="tpu_custom_call" | custom-call | tf_op jit(solution)/shard_map/transforms/pallas_call | solution.py:248
  44.5 14.3 %exchange_tm.1.products_ref = bf16[8,3,128,128]{3,2,1,0:T(8,128)(2,1)} custom-call(bf16[3,128,128]{2,1,0:T(8,128)(2,1)} %get-tuple-element.11.refs_0_), custom_call_target="tpu_custom_call" | custom-call | tf_op jit(solution)/shard_map/exchange_tm/pallas_call | solution.py:216
  58.8 4.6 %fold.1.weight_ref = bf16[3,256,256]{2,1,0:T(8,128)(2,1)} custom-call(s32[1]{0:T(128)} %bitcast.1.position_ref, bf16[8,3,128,128]{3,2,1,0:T(8,128)(2,1)} %exchange_tm.1.products_ref, f32[3,256,256]{2,1,0:T(8,128)} %get-tuple-element.12.partial_ref), custom_call_target="tpu_custom_call" | custom-call | tf_op jit(solution)/shard_map/fold/pallas_call | solution.py:261
  63.4 8.0 %apply.1 = bf16[3,4096,256]{2,1,0:T(8,128)(2,1)} custom-call(bf16[3,4096,256]{2,1,0:T(8,128)(2,1)} %bitcast.15, bf16[3,256,256]{2,1,0:T(8,128)(2,1)} %fold.1.weight_ref), custom_call_target="tpu_custom_call" | custom-call | tf_op jit(solution)/shard_map/apply/pallas_call | solution.py:271
where the time goes:
time: 71.9 us; the launch traced here: 71.5 us
  Pallas kernels  65.1 us (91%)
  local copies, waits for them, and re-layouts  4.34 us (6%)
  other arithmetic  2.02 us (3%)
    pallas_call x2, Pallas kernels, exchange(): pl.pallas_call(lambda *refs: exchange_kernel(axis, count, one_way, items,...  26.3 us
    pallas_call x1, Pallas kernels, local(): pl.pallas_call(transforms_kernel, out_shape=(jax.ShapeDtypeStruct((window...  26.1 us
    pallas_call x1, Pallas kernels, local(): pl.pallas_call(apply_kernel, out_shape=jax.ShapeDtypeStruct(flat.shape, B...  8.01 us
    pallas_call x1, Pallas kernels, local(): pl.pallas_call(fold_kernel, out_shape=jax.ShapeDtypeStruct((windows, memb...  4.61 us
    gather x2, local copies, waits for them, and re-layouts, local(): field[0][where_at]  2.24 us
    squeeze x1, local copies, waits for them, and re-layouts, local(): field[0][where_at]  2.09 us

commit v1 on v0

--- a/solution.py
+++ b/solution.py
@@ -7,6 +7,9 @@
 
 F32 = jnp.float32
 BF16 = jnp.bfloat16
+SPREAD_GAIN = 1.4
+SETTLED = 4e-4
+MIB = 1 << 20
 
 
 def dot_any(left, right, dims):
@@ -79,8 +82,12 @@
     return results
 
 
+def lower_half(value, row, col):
+    return jnp.where(row > col, value, jnp.where(row == col, 0.5 * value, 0.0))
+
+
 def transforms_kernel(
-    rho_ref, picked_ref, weight_ref, partial_ref, own_ref, gram, first_inv, second_inv, low_ref, mid_ref
+    rho_ref, picked_ref, weight_ref, partial_ref, own_ref, high_ref, low_ref, x_ref, first_inv, second_inv, mid_ref
 ):
     blocks, windows, slots, members = picked_ref.shape
     half = members // 2
@@ -88,25 +95,84 @@
         lax.broadcasted_iota(jnp.int32, (slots, slots), 0)
         == lax.broadcasted_iota(jnp.int32, (slots, slots), 1)
     )
-    eye = (
-        lax.broadcasted_iota(jnp.int32, (members, members), 0)
-        == lax.broadcasted_iota(jnp.int32, (members, members), 1)
-    )
+    row = lax.broadcasted_iota(jnp.int32, (members, members), 0)
+    col = lax.broadcasted_iota(jnp.int32, (members, members), 1)
+    eye = row == col
+    nn = ((1,), (0,))
     tn = ((0,), (0,))
     nt = ((1,), (1,))
 
-    @pl.loop(0, windows)
-    def _(w):
+    for w in range(windows):
         rows = jnp.concatenate([picked_ref[n, w] for n in range(blocks)], axis=0)
         columns = [
-            jnp.sum(
-                jnp.where(slot_eye, weight_ref[n, pl.ds(w, 1), :], 0.0), axis=1, keepdims=True
-            )
+            jnp.sum(jnp.where(slot_eye, weight_ref[n, w : w + 1, :], 0.0), axis=1, keepdims=True)
             for n in range(blocks)
         ]
         high, low = halves(rows.astype(F32) * jnp.concatenate(columns, axis=0))
-        total = dot_any(high, rows, tn) + dot_any(low, rows, tn)
-        gram[w] = total + jnp.where(eye, F32(members - 1.0), 0.0)
+        system = dot_any(high, rows, tn) + dot_any(low, rows, tn) + jnp.where(eye, F32(members - 1.0), 0.0)
+        high_ref[w], low_ref[w] = halves(system)
+        diagonal = jnp.where(eye, system, 0.0)
+        scale_row = lax.rsqrt(jnp.sum(diagonal, axis=0, keepdims=True))
+        scale_col = lax.rsqrt(jnp.sum(diagonal, axis=1, keepdims=True))
+        corr = system * scale_col * scale_row
+        off = jnp.where(eye, 0.0, corr)
+        spread = jnp.sum(jnp.sum(off * off, axis=0, keepdims=True), axis=1, keepdims=True)
+        beta = 1.0 / (1.0 + SPREAD_GAIN * jnp.sqrt(spread * (1.0 / members)))
+        change = lower_half(beta * corr - jnp.where(eye, 1.0, 0.0), row, col)
+        narrow = change.astype(BF16)
+        second = dot_any(narrow, narrow, nn) + lower_half(dot_any(narrow, narrow, nt), row, col)
+        unit = jnp.where(eye, 1.0, 0.0) - change + second
+        x_ref[w] = unit * (scale_row * jnp.sqrt(beta))
+
+    def refine(state):
+        turn, _ = state
+        worst = jnp.zeros((1, 1), F32)
+        for w in range(windows):
+            x = x_ref[w]
+            xh, xl = halves(x)
+            ah = high_ref[w]
+            left = dot_any(xh, ah, nn) + (dot_any(xh, low_ref[w], nn) + dot_any(xl, ah, nn))
+            lh, ll = halves(left)
+            near = dot_any(lh, xh, nt) + (dot_any(lh, xl, nt) + dot_any(ll, xh, nt))
+            change = lower_half(near - jnp.where(eye, 1.0, 0.0), row, col)
+            size = jnp.sum(jnp.sum(change * change, axis=0, keepdims=True), axis=1, keepdims=True)
+            worst = jnp.where(size <= worst, worst, size)
+            narrow = change.astype(BF16)
+            square = lower_half(dot_any(narrow, narrow, nt), row, col).astype(BF16)
+            rest = (x - dot_any(narrow, xh, nn)).astype(BF16)
+            x_ref[w] = x - dot_any(narrow, rest, nn) + dot_any(square, xh, nn)
+        return turn + 1, worst[0, 0]
+
+    def again(state):
+        turn, size = state
+        return (turn < 8) & (size > SETTLED) & (size < 1.0)
+
+    _, size = lax.while_loop(again, refine, refine((jnp.int32(0), F32(0.5))))
+
+    @pl.when(jnp.logical_not(size <= SETTLED))
+    def _():
+        direct(high_ref, low_ref, partial_ref, x_ref, first_inv, second_inv, mid_ref)
+
+    for w in range(windows):
+        scale = rho_ref[w] * jnp.sqrt(F32(members - 1.0))
+        partial_ref[w] = scale * x_ref[w]
+
+    for turn in range(windows - 1):
+        w = windows - 2 - turn
+        partial_ref[w] = dot_three(partial_ref[w + 1], partial_ref[w])
+
+    own_ref[0] = partial_ref[0, :half, :half].astype(BF16)
+    own_ref[1] = partial_ref[0, half:, :half].astype(BF16)
+    own_ref[2] = partial_ref[0, half:, half:].astype(BF16)
+
+
+def direct(high_ref, low_ref, gram, x_ref, first_inv, second_inv, mid_ref):
+    windows, members, _ = x_ref.shape
+    half = members // 2
+    nt = ((1,), (1,))
+
+    for w in range(windows):
+        gram[w] = high_ref[w].astype(F32) + low_ref[w].astype(F32)
 
     for w, value in enumerate(eliminate([gram[w, :half, :half] for w in range(windows)])):
         first_inv[w] = value
@@ -114,32 +180,18 @@
     @pl.loop(0, windows)
     def _(w):
         lower = dot_full(gram[w, half:, :half], first_inv[w], nt)
-        low_ref[w] = lower
         gram[w, half:, half:] -= dot_full(lower, lower, nt)
         mid_ref[w] = dot_full(lower, first_inv[w])
 
     for w, value in enumerate(eliminate([gram[w, half:, half:] for w in range(windows)])):
         second_inv[w] = value
 
-    zero = jnp.zeros((half, half), F32)
-
     @pl.loop(0, windows)
     def _(w):
-        scale = rho_ref[w] * jnp.sqrt(F32(members - 1.0))
-        cross = -dot_full(second_inv[w], mid_ref[w])
-        partial_ref[w, :half, :half] = scale * first_inv[w].T
-        partial_ref[w, :half, half:] = scale * cross.T
-        partial_ref[w, half:, :half] = zero
-        partial_ref[w, half:, half:] = scale * second_inv[w].T
-
-    @pl.loop(0, windows - 1)
-    def _(turn):
-        w = windows - 2 - turn
-        partial_ref[w] = dot_three(partial_ref[w], partial_ref[w + 1])
-
-    own_ref[0] = partial_ref[0, :half, :half].astype(BF16)
-    own_ref[1] = partial_ref[0, :half, half:].astype(BF16)
-    own_ref[2] = partial_ref[0, half:, half:].astype(BF16)
+        x_ref[w, :half, :half] = first_inv[w]
+        x_ref[w, :half, half:] = jnp.zeros((half, half), F32)
+        x_ref[w, half:, :half] = -dot_full(second_inv[w], mid_ref[w])
+        x_ref[w, half:, half:] = second_inv[w]
 
 
 def fold_kernel(position_ref, products_ref, partial_ref, out_ref, whole, later):
@@ -157,15 +209,15 @@
     def _(turn):
         source = count - 1 - turn
         whole[:half, :half] = products_ref[source, 0]
-        whole[:half, half:] = products_ref[source, 1]
+        whole[half:, :half] = products_ref[source, 1]
         whole[half:, half:] = products_ref[source, 2]
         high, low = halves(later[...])
-        left = whole[...]
-        later[...] = dot_any(left, high, ((1,), (0,))) + dot_any(left, low, ((1,), (0,)))
+        right = whole[...]
+        later[...] = dot_any(high, right, ((1,), (0,))) + dot_any(low, right, ((1,), (0,)))
 
     @pl.loop(0, windows)
     def _(w):
-        out_ref[w] = dot_three(partial_ref[w], later[...]).astype(BF16)
+        out_ref[w] = dot_three(later[...], partial_ref[w]).astype(BF16)
 
 
 def exchange_kernel(axis, count, one_way, items, *refs):
@@ -222,15 +274,16 @@
             pltpu.SemaphoreType.DMA((items, count)),
             pltpu.SemaphoreType.DMA((items, count)),
         ],
-        compiler_params=pltpu.CompilerParams(collective_id=collective_id, has_side_effects=True),
+        compiler_params=pltpu.CompilerParams(
+            collective_id=collective_id, has_side_effects=True, vmem_limit_bytes=8 * MIB
+        ),
+        cost_estimate=pl.CostEstimate(flops=2 * 10**9, bytes_accessed=MIB, transcendentals=0),
         name="exchange_" + axis,
     )(*values)
 
 
 def apply_kernel(field_ref, weight_ref, out_ref):
-    out_ref[0] = jnp.dot(field_ref[0], weight_ref[0], preferred_element_type=F32).astype(
-        out_ref.dtype
-    )
+    out_ref[0] = dot_any(field_ref[0], weight_ref[0], ((1,), (1,))).astype(out_ref.dtype)
 
 
 def local(anomalies, obs_cells, obs_counts, obs_precision, inflation):
@@ -253,8 +306,11 @@
         ),
         in_specs=[smem, vmem, vmem],
         out_specs=(vmem, vmem),
-        scratch_shapes=[pltpu.VMEM((windows, members, members), F32)]
-        + [pltpu.VMEM((windows, half, half), F32)] * 4,
+        scratch_shapes=[pltpu.VMEM((windows, members, members), BF16)] * 2
+        + [pltpu.VMEM((windows, members, members), F32)]
+        + [pltpu.VMEM((windows, half, half), F32)] * 3,
+        compiler_params=pltpu.CompilerParams(vmem_limit_bytes=16 * MIB),
+        cost_estimate=pl.CostEstimate(flops=4 * 10**9, bytes_accessed=2 * MIB, transcendentals=0),
         name="transforms",
     )(inflation, gathered, gathered_weights)
     (products,) = exchange("tm", True, 1, own)
@@ -264,6 +320,8 @@
         in_specs=[smem, vmem, vmem],
         out_specs=vmem,
         scratch_shapes=[pltpu.VMEM((members, members), BF16), pltpu.VMEM((members, members), F32)],
+        compiler_params=pltpu.CompilerParams(vmem_limit_bytes=8 * MIB),
+        cost_estimate=pl.CostEstimate(flops=10**9, bytes_accessed=MIB, transcendentals=0),
         name="fold",
     )(lax.axis_index("tm").astype(jnp.int32)[None], products, partial)
     flat = anomalies.reshape(windows, 2 * cell_width, members)
@@ -277,6 +335,7 @@
             pl.BlockSpec((1, members, members), lambda w, c: (w, 0, 0)),
         ],
         out_specs=pl.BlockSpec((1, tile, members), lambda w, c: (w, c, 0)),
+        compiler_params=pltpu.CompilerParams(vmem_limit_bytes=16 * MIB),
         name="apply",
     )(flat, weight_mats)
     return result.reshape(anomalies.shape)

time: 71.9 us -> 63.6 us (0.88)
  Pallas kernels: 65.1 us -> 58.2 us
    pallas_call x1, Pallas kernels: 8.01 us -> 4.82 us  [local(): pl.pallas_call(apply_kernel, out_shape=jax.ShapeDtypeStruct(flat.shape, B...]
    pallas_call x2, Pallas kernels: 26.3 us -> 23.3 us  [exchange(): pl.pallas_call(lambda *refs: exchange_kernel(axis, count, one_way, items,...]
    pallas_call x1, Pallas kernels: 4.61 us -> 2.6 us  [local(): pl.pallas_call(fold_kernel, out_shape=jax.ShapeDtypeStruct((windows, memb...]
    pallas_call x1, Pallas kernels: 26.1 us -> 27.5 us  [local(): pl.pallas_call(transforms_kernel, out_shape=(jax.ShapeDtypeStruct((window...]
where the time goes in v1:
time: 63.6 us; the launch traced here: 63.4 us
  Pallas kernels  58.2 us (92%)
  local copies, waits for them, and re-layouts  3.68 us (6%)
  other arithmetic  1.44 us (2%)
    pallas_call x1, Pallas kernels, local(): pl.pallas_call(transforms_kernel, out_shape=(jax.ShapeDtypeStruct((window...  27.5 us
    pallas_call x2, Pallas kernels, exchange(): pl.pallas_call(lambda *refs: exchange_kernel(axis, count, one_way, items,...  23.3 us
    pallas_call x1, Pallas kernels, local(): pl.pallas_call(apply_kernel, out_shape=jax.ShapeDtypeStruct(flat.shape, B...  4.82 us
    pallas_call x1, Pallas kernels, local(): pl.pallas_call(fold_kernel, out_shape=jax.ShapeDtypeStruct((windows, memb...  2.6 us
    squeeze x1, local copies, waits for them, and re-layouts, local(): field[0][where_at]  2.11 us
    gather x2, local copies, waits for them, and re-layouts, local(): field[0][where_at]  1.56 us

profile of v1, /device:TPU:0, one launch (start us, length us, event | category | flops | bytes accessed | tf_op | source)
XLA Modules:
  0.0 63.4 jit_solution(2168873595657627534)
XLA Ops:
  0.0 0.7 %fusion.3 = s32[3,32,1]{1,0,2:T(4,128)S(1)} fusion(s32[3,32]{1,0:T(4,128)} %param.6, s32[]{:T(128)S(6)} %mul.3), kind=kLoop, calls=%fused_computation.6 | loop fusion | flops 864 | bytes 772 | tf_op jit(solution)/shard_map/vmap()/gather | solution.py:295
  0.7 0.1 reshape.8
  0.8 0.8 %fusion.4.refs_1_ = f32[3,32]{1,0:T(4,128)S(1)} fusion(f32[3,32]{1,0:T(4,128)} %param.8, s32[3]{0:T(128)} %bitcast.19), kind=kLoop, calls=%fused_computation.8 | loop fusion | flops 192 | bytes 780 | tf_op jit(solution)/shard_map/jit(_where)/select_n | solution.py:297
  1.5 0.0 copy-start
  1.5 2.1 %slice_bitcast_fusion = bf16[3,2048,256]{2,1,0:T(8,128)(2,1)S(1)} fusion(bf16[3,2,2048,256]{3,2,1,0:T(8,128)(2,1)} %param.5), kind=kLoop, calls=%fused_computation.1 | loop fusion | bytes 6291456 | tf_op jit(solution)/shard_map/vmap()/squeeze | solution.py:295
  3.6 1.5 %gather_fusion = bf16[96,256]{1,0:T(8,128)(2,1)S(1)} fusion(bf16[3,2048,256]{2,1,0:T(8,128)(2,1)S(1)} %slice_bitcast_fusion, s32[96]{0:T(128)S(1)} %reshape.8), kind=kCustom, calls=%fused_computation | custom fusion | bytes 99072 | tf_op jit(solution)/shard_map/vmap()/gather | solution.py:295
  5.1 10.6 %exchange_cell.1 = (bf16[4,3,32,256]{3,2,1,0:T(8,128)(2,1)S(1)}, f32[4,3,32]{2,1,0:T(4,128)S(1)}) custom-call(bf16[3,32,256]{2,1,0:T(8,128)(2,1)S(1)} %bitcast.18, f32[3,32]{1,0:T(4,128)S(1)} %fusion.4.refs_1_), custom_call_target="tpu_custom_call" | custom-call | flops 2000000000 | bytes 1048576 | tf_op jit(solution)/shard_map/exchange_cell/pallas_call | solution.py:268
  15.7 0.0 slice-start
  15.8 0.0 copy-done
  15.8 0.0 slice-start.1
  15.8 27.5 %transforms.1 = (f32[3,256,256]{2,1,0:T(8,128)S(1)}, bf16[3,128,128]{2,1,0:T(8,128)(2,1)S(1)}) custom-call(f32[3]{0:T(128)S(1)} %copy-done, bf16[4,3,32,256]{3,2,1,0:T(8,128)(2,1)S(1)} %get-tuple-element.9.picked_ref, f32[4,3,32]{2,1,0:T(4,128)S(1)} %get-tuple-element.10.weight_ref), custom_call_target="tpu_custom_call" | custom-call | flops 4000000000 | bytes 2097152 | tf_op jit(solution)/shard_map/transforms/pallas_call | solution.py:301
  43.3 12.6 %exchange_tm.1.products_ref = bf16[8,3,128,128]{3,2,1,0:T(8,128)(2,1)S(1)} custom-call(bf16[3,128,128]{2,1,0:T(8,128)(2,1)S(1)} %get-tuple-element.11.refs_0_), custom_call_target="tpu_custom_call" | custom-call | flops 2000000000 | bytes 1048576 | tf_op jit(solution)/shard_map/exchange_tm/pallas_call | solution.py:268
  55.9 2.6 %fold.1.weight_ref = bf16[3,256,256]{2,1,0:T(8,128)(2,1)S(1)} custom-call(s32[1]{0:T(128)} %bitcast.1.position_ref, bf16[8,3,128,128]{3,2,1,0:T(8,128)(2,1)S(1)} %exchange_tm.1.products_ref, f32[3,256,256]{2,1,0:T(8,128)S(1)} %get-tuple-element.12.partial_ref), custom_call_target="tpu_custom_call" | custom-call | flops 1000000000 | bytes 1048576 | tf_op jit(solution)/shard_map/fold/pallas_call | solution.py:317
  58.5 0.0 slice-done
  58.5 0.0 slice-done.1
  58.6 4.8 %apply.1 = bf16[3,4096,256]{2,1,0:T(8,128)(2,1)} custom-call(bf16[3,4096,256]{2,1,0:T(8,128)(2,1)S(1)} %bitcast.17, bf16[3,256,256]{2,1,0:T(8,128)(2,1)S(1)} %fold.1.weight_ref), custom_call_target="tpu_custom_call" | custom-call | tf_op jit(solution)/shard_map/apply/pallas_call | solution.py:329
  (1 shorter events, 0.0 us)
Async XLA Ops:
  1.5 14.2 %copy-start = (f32[3]{0:T(128)S(1)}, f32[3]{0:T(128)}, u32[]{:S(2)}) copy-start(f32[3]{0:T(128)} %rho_ref.1) | copy-start | bytes 40
  15.7 42.8 %slice-start = ((s8[6291456]{0:T(1024)(128)(4,1)}), s8[4194304]{0:T(1024)(128)(4,1)S(1)}, s32[]{:S(2)}) async-start(s8[6291456]{0:T(1024)(128)(4,1)} %bitcast.15), calls=%async_computation | async-start | bytes 8388608
  15.8 42.8 %slice-start.1 = ((s8[6291456]{0:T(1024)(128)(4,1)}), s8[2097152]{0:T(1024)(128)(4,1)S(1)}, s32[]{:S(2)}) async-start(s8[6291456]{0:T(1024)(128)(4,1)} %bitcast.15), calls=%async_computation.1 | async-start | bytes 4194304

commit v2 on v1

--- a/solution.py
+++ b/solution.py
@@ -194,32 +194,6 @@
         x_ref[w, half:, half:] = second_inv[w]
 
 
-def fold_kernel(position_ref, products_ref, partial_ref, out_ref, whole, later):
-    count = products_ref.shape[0]
-    windows, members, _ = partial_ref.shape
-    half = members // 2
-    position = position_ref[0]
-    whole[...] = jnp.zeros_like(whole)
-    later[...] = (
-        lax.broadcasted_iota(jnp.int32, (members, members), 0)
-        == lax.broadcasted_iota(jnp.int32, (members, members), 1)
-    ).astype(F32)
-
-    @pl.loop(0, count - 1 - position)
-    def _(turn):
-        source = count - 1 - turn
-        whole[:half, :half] = products_ref[source, 0]
-        whole[half:, :half] = products_ref[source, 1]
-        whole[half:, half:] = products_ref[source, 2]
-        high, low = halves(later[...])
-        right = whole[...]
-        later[...] = dot_any(high, right, ((1,), (0,))) + dot_any(low, right, ((1,), (0,)))
-
-    @pl.loop(0, windows)
-    def _(w):
-        out_ref[w] = dot_three(later[...], partial_ref[w]).astype(BF16)
-
-
 def exchange_kernel(axis, count, one_way, items, *refs):
     ins, outs = refs[:items], refs[items : 2 * items]
     send_sem, recv_sem = refs[2 * items :]
@@ -282,22 +256,172 @@
     )(*values)
 
 
-def apply_kernel(field_ref, weight_ref, out_ref):
-    out_ref[0] = dot_any(field_ref[0], weight_ref[0], ((1,), (1,))).astype(out_ref.dtype)
+def observe_kernel(axis, count, chunk, field_ref, cells_hbm, counts_hbm, precision_hbm,
+    rows_ref, weights_ref, dens, cells_ref, counts_ref, precision_ref, small_sem, load_sem, send_sem, recv_sem):
+    windows, slots = cells_ref.shape
+    depth = dens.shape[1]
+    pieces = depth // chunk
+    me = lax.axis_index(axis)
+
+    def load_of(w, piece):
+        span = pl.ds(piece * chunk, chunk)
+        return pltpu.make_async_copy(
+            field_ref.at[w, 0, span, :], dens.at[w, span, :], load_sem.at[w, piece]
+        )
+
+    small = [
+        pltpu.make_async_copy(source, target, small_sem.at[i])
+        for i, (source, target) in enumerate(
+            ((cells_hbm, cells_ref), (counts_hbm, counts_ref), (precision_hbm, precision_ref))
+        )
+    ]
+    for copy in small:
+        copy.start()
+    for w in range(windows):
+        for piece in range(pieces):
+            load_of(w, piece).start()
+    barrier = pltpu.get_barrier_semaphore()
+    for shift in range(1, count):
+        pl.semaphore_signal(
+            barrier,
+            inc=1,
+            device_id={axis: lax.rem(me + shift, count)},
+            device_id_type=pl.DeviceIdType.MESH,
+        )
+
+    def copy_of(shift, item, source, target):
+        return pltpu.make_async_remote_copy(
+            src_ref=source,
+            dst_ref=target,
+            send_sem=send_sem.at[item, shift],
+            recv_sem=recv_sem.at[item, shift],
+            device_id={axis: lax.rem(me + count - shift, count)},
+            device_id_type=pl.DeviceIdType.MESH,
+        )
+
+    def rows_copy(shift, w):
+        return copy_of(shift, w, rows_ref.at[me, w], rows_ref.at[me, w])
+
+    def weights_copy(shift):
+        return copy_of(shift, windows, weights_ref.at[me], weights_ref.at[me])
+
+    for copy in small:
+        copy.wait()
+    slot = lax.broadcasted_iota(jnp.int32, (windows, slots), 1)
+    window = lax.broadcasted_iota(jnp.int32, (windows, slots), 0)
+    counts = jnp.zeros((windows, slots), jnp.int32)
+    for w in range(windows):
+        counts = jnp.where(window == w, counts_ref[w], counts)
+    weights_ref[me] = jnp.where(slot < counts, precision_ref[...], 0.0)
+    slot_eye = (
+        lax.broadcasted_iota(jnp.int32, (slots, slots), 0)
+        == lax.broadcasted_iota(jnp.int32, (slots, slots), 1)
+    )
+    place = lax.broadcasted_iota(jnp.int32, (slots, chunk), 1)
+    offsets = (cells_ref[...] - me * depth).astype(F32)
+    columns = [
+        jnp.sum(jnp.where(slot_eye, offsets[w : w + 1, :], 0.0), axis=1, keepdims=True).astype(
+            jnp.int32
+        )
+        for w in range(windows)
+    ]
+    for w in range(windows):
+        total = jnp.zeros((slots, dens.shape[2]), F32)
+        for piece in range(pieces):
+            hit = jnp.where(place + piece * chunk == columns[w], 1.0, 0.0).astype(BF16)
+            load_of(w, piece).wait()
+            total += dot_any(hit, dens[w, pl.ds(piece * chunk, chunk), :], ((1,), (0,)))
+        rows_ref[me, w] = total.astype(BF16)
+        if w == 0:
+            pl.semaphore_wait(barrier, count - 1)
+            for shift in range(1, count):
+                weights_copy(shift).start()
+        for shift in range(1, count):
+            rows_copy(shift, w).start()
+    for shift in range(1, count):
+        weights_copy(shift).wait()
+        for w in range(windows):
+            rows_copy(shift, w).wait()
+
+
+def apply_kernel(position_ref, field_ref, products_ref, partial_ref, out_ref, whole, later, stage, sems):
+    count = products_ref.shape[0]
+    windows, height, members = field_ref.shape
+    half = members // 2
+    tile = stage.shape[2]
+    tiles = height // tile
+    nn = ((1,), (0,))
+    whole[...] = jnp.zeros_like(whole)
+    later[...] = (
+        lax.broadcasted_iota(jnp.int32, (members, members), 0)
+        == lax.broadcasted_iota(jnp.int32, (members, members), 1)
+    ).astype(F32)
+
+    @pl.loop(0, count - 1 - position_ref[0])
+    def _(turn):
+        source = count - 1 - turn
+        whole[:half, :half] = products_ref[source, 0]
+        whole[half:, :half] = products_ref[source, 1]
+        whole[half:, half:] = products_ref[source, 2]
+        high, low = halves(later[...])
+        right = whole[...]
+        later[...] = dot_any(high, right, nn) + dot_any(low, right, nn)
+
+    def out_of(w, t):
+        return pltpu.make_async_copy(
+            stage.at[w, t], out_ref.at[w, pl.ds(t * tile, tile), :], sems.at[w, t]
+        )
+
+    for w in range(windows):
+        weight = dot_three(later[...], partial_ref[w]).astype(BF16)
+        for t in range(tiles):
+            stage[w, t] = dot_any(
+                field_ref[w, pl.ds(t * tile, tile), :], weight, ((1,), (1,))
+            ).astype(BF16)
+            out_of(w, t).start()
+    for w in range(windows):
+        for t in range(tiles):
+            out_of(w, t).wait()
 
 
 def local(anomalies, obs_cells, obs_counts, obs_precision, inflation):
-    windows, _, cell_width, members = anomalies.shape
+    windows, fields, cell_width, members = anomalies.shape
     half = members // 2
     slots = obs_cells.shape[1]
-    first_cell = lax.axis_index("cell") * cell_width
-    offsets = obs_cells - first_cell
-    picked = jax.vmap(lambda field, where_at: field[0][where_at])(anomalies, offsets)
-    live = jnp.arange(slots, dtype=jnp.int32)[None, :] < obs_counts
-    weights = jnp.where(live, obs_precision, jnp.float32(0.0))
-    gathered, gathered_weights = exchange("cell", False, 0, picked, weights)
+    count = lax.axis_size("cell")
+    chunk = min(1024, cell_width)
     vmem = pl.BlockSpec(memory_space=pltpu.VMEM)
     smem = pl.BlockSpec(memory_space=pltpu.SMEM)
+    hbm = pl.BlockSpec(memory_space=pltpu.HBM)
+    gathered, gathered_weights = pl.pallas_call(
+        lambda *refs: observe_kernel("cell", count, chunk, *refs),
+        out_shape=(
+            jax.ShapeDtypeStruct((count, windows, slots, members), BF16),
+            jax.ShapeDtypeStruct((count, windows, slots), F32),
+        ),
+        in_specs=[hbm] * 4,
+        out_specs=(vmem, vmem),
+        scratch_shapes=[
+            pltpu.VMEM((windows, cell_width, members), BF16),
+            pltpu.VMEM((windows, slots), jnp.int32),
+            pltpu.SMEM((windows,), jnp.int32),
+            pltpu.VMEM((windows, slots), F32),
+            pltpu.SemaphoreType.DMA((3,)),
+            pltpu.SemaphoreType.DMA((windows, cell_width // chunk)),
+            pltpu.SemaphoreType.DMA((windows + 1, count)),
+            pltpu.SemaphoreType.DMA((windows + 1, count)),
+        ],
+        compiler_params=pltpu.CompilerParams(
+            collective_id=0, has_side_effects=True, vmem_limit_bytes=12 * MIB
+        ),
+        cost_estimate=pl.CostEstimate(flops=2 * 10**9, bytes_accessed=MIB, transcendentals=0),
+        name="observe",
+    )(
+        *(
+            pltpu.with_memory_space_constraint(value, pltpu.HBM)
+            for value in (anomalies, obs_cells, obs_counts.reshape(windows), obs_precision)
+        )
+    )
     partial, own = pl.pallas_call(
         transforms_kernel,
         out_shape=(
@@ -314,30 +438,22 @@
         name="transforms",
     )(inflation, gathered, gathered_weights)
     (products,) = exchange("tm", True, 1, own)
-    weight_mats = pl.pallas_call(
-        fold_kernel,
-        out_shape=jax.ShapeDtypeStruct((windows, members, members), BF16),
-        in_specs=[smem, vmem, vmem],
-        out_specs=vmem,
-        scratch_shapes=[pltpu.VMEM((members, members), BF16), pltpu.VMEM((members, members), F32)],
-        compiler_params=pltpu.CompilerParams(vmem_limit_bytes=8 * MIB),
-        cost_estimate=pl.CostEstimate(flops=10**9, bytes_accessed=MIB, transcendentals=0),
-        name="fold",
-    )(lax.axis_index("tm").astype(jnp.int32)[None], products, partial)
-    flat = anomalies.reshape(windows, 2 * cell_width, members)
-    tile = min(2048, 2 * cell_width)
+    flat = anomalies.reshape(windows, fields * cell_width, members)
+    tile = min(512, cell_width)
     result = pl.pallas_call(
         apply_kernel,
         out_shape=jax.ShapeDtypeStruct(flat.shape, BF16),
-        grid=(windows, 2 * cell_width // tile),
-        in_specs=[
-            pl.BlockSpec((1, tile, members), lambda w, c: (w, c, 0)),
-            pl.BlockSpec((1, members, members), lambda w, c: (w, 0, 0)),
+        in_specs=[smem, vmem, vmem, vmem],
+        out_specs=hbm,
+        scratch_shapes=[
+            pltpu.VMEM((members, members), BF16),
+            pltpu.VMEM((members, members), F32),
+            pltpu.VMEM((windows, fields * cell_width // tile, tile, members), BF16),
+            pltpu.SemaphoreType.DMA((windows, fields * cell_width // tile)),
         ],
-        out_specs=pl.BlockSpec((1, tile, members), lambda w, c: (w, c, 0)),
         compiler_params=pltpu.CompilerParams(vmem_limit_bytes=16 * MIB),
         name="apply",
-    )(flat, weight_mats)
+    )(lax.axis_index("tm").astype(jnp.int32)[None], flat, products, partial)
     return result.reshape(anomalies.shape)
 
 

time: 63.6 us -> 57.8 us (0.909)
  local copies, waits for them, and re-layouts: 3.68 us -> 0.02 us
  other arithmetic: 1.44 us -> 0.01 us
  Pallas kernels: 58.2 us -> 57.4 us
    pallas_call x2 -> x1, Pallas kernels: 23.3 us -> 12.6 us  [exchange(): pl.pallas_call(lambda *refs: exchange_kernel(axis, count, one_way, items,...]
    pallas_call x1, Pallas kernels: 2.6 us -> 11.5 us  [local(): pl.pallas_call(lambda *refs: observe_kernel('cell', count, chunk, *refs),...]
    squeeze x1 -> x0, local copies, waits for them, and re-layouts: 2.11 us -> none  [local(): field[0][where_at]]
    gather x2 -> x0, local copies, waits for them, and re-layouts: 1.56 us -> none  [local(): field[0][where_at]]
    pallas_call x1, Pallas kernels: 4.82 us -> 5.72 us  [local(): pl.pallas_call(apply_kernel, out_shape=jax.ShapeDtypeStruct(flat.shape, B...]
    select_n x1 -> x0, other arithmetic: 0.75 us -> none  [local(): weights = jnp.where(live, obs_precision, jnp.float32(0.0))]
    gather x1 -> x0, other arithmetic: 0.69 us -> none  [local(): field[0][where_at]]
where the time goes in v2:
time: 57.8 us; the launch traced here: 57.6 us
  Pallas kernels  57.4 us (99%)
    pallas_call x1, Pallas kernels, local(): pl.pallas_call(transforms_kernel, out_shape=(jax.ShapeDtypeStruct((window...  27.5 us
    pallas_call x1, Pallas kernels, exchange(): pl.pallas_call(lambda *refs: exchange_kernel(axis, count, one_way, items,...  12.6 us
    pallas_call x1, Pallas kernels, local(): pl.pallas_call(lambda *refs: observe_kernel('cell', count, chunk, *refs),...  11.5 us
    pallas_call x1, Pallas kernels, local(): pl.pallas_call(apply_kernel, out_shape=jax.ShapeDtypeStruct(flat.shape, B...  5.72 us

profile of v2, /device:TPU:0, one launch (start us, length us, event | category | flops | bytes accessed | tf_op | source)
XLA Modules:
  0.0 57.6 jit_solution(3648663536158176480)
XLA Ops:
  0.0 0.0 copy-start
  0.0 11.5 %observe.1 = (bf16[4,3,32,256]{3,2,1,0:T(8,128)(2,1)S(1)}, f32[4,3,32]{2,1,0:T(4,128)S(1)}) custom-call(bf16[3,2,2048,256]{3,2,1,0:T(8,128)(2,1)} %refs_0_.1, s32[3,32]{1,0:T(4,128)} %refs_1_.1, s32[3]{0:T(128)} %bitcast.7, f32[3,32]{1,0:T(4,128)} %refs_3_.1), custom_call_target="tpu_custom_call" | custom-call | flops 2000000000 | bytes 1048576 | tf_op jit(solution)/shard_map/observe/pallas_call | solution.py:396
  11.5 0.0 slice-start
  11.5 0.0 copy-done
  11.6 0.0 slice-start.1
  11.6 27.5 %transforms.1 = (f32[3,256,256]{2,1,0:T(8,128)S(1)}, bf16[3,128,128]{2,1,0:T(8,128)(2,1)S(1)}) custom-call(f32[3]{0:T(128)S(1)} %copy-done, bf16[4,3,32,256]{3,2,1,0:T(8,128)(2,1)S(1)} %get-tuple-element.9.picked_ref, f32[4,3,32]{2,1,0:T(4,128)S(1)} %get-tuple-element.10.weight_ref), custom_call_target="tpu_custom_call" | custom-call | flops 4000000000 | bytes 2097152 | tf_op jit(solution)/shard_map/transforms/pallas_call | solution.py:425
  39.1 12.6 %exchange_tm.1.products_ref = bf16[8,3,128,128]{3,2,1,0:T(8,128)(2,1)S(1)} custom-call(bf16[3,128,128]{2,1,0:T(8,128)(2,1)S(1)} %get-tuple-element.11.refs_0_), custom_call_target="tpu_custom_call" | custom-call | flops 2000000000 | bytes 1048576 | tf_op jit(solution)/shard_map/exchange_tm/pallas_call | solution.py:242
  51.7 0.0 slice-done
  51.7 0.0 slice-done.1
  51.7 5.7 %apply.1 = bf16[3,4096,256]{2,1,0:T(8,128)(2,1)} custom-call(s32[1]{0:T(128)} %bitcast.position_ref, bf16[3,4096,256]{2,1,0:T(8,128)(2,1)S(1)} %bitcast.6, bf16[8,3,128,128]{3,2,1,0:T(8,128)(2,1)S(1)} %exchange_tm.1.products_ref, f32[3,256,256]{2,1,0:T(8,128)S(1)} %get-tuple-element.12.partial_ref), custom_call_target="tpu_custom_call" | custom-call | tf_op jit(solution)/shard_map/apply/pallas_call | solution.py:443
  (1 shorter events, 0.0 us)
Async XLA Ops:
  0.0 11.5 %copy-start = (f32[3]{0:T(128)S(1)}, f32[3]{0:T(128)}, u32[]{:S(2)}) copy-start(f32[3]{0:T(128)} %rho_ref.1) | copy-start | bytes 40
  11.5 40.2 %slice-start = ((s8[6291456]{0:T(1024)(128)(4,1)}), s8[4194304]{0:T(1024)(128)(4,1)S(1)}, s32[]{:S(2)}) async-start(s8[6291456]{0:T(1024)(128)(4,1)} %bitcast.4), calls=%async_computation | async-start | bytes 8388608
  11.6 40.2 %slice-start.1 = ((s8[6291456]{0:T(1024)(128)(4,1)}), s8[2097152]{0:T(1024)(128)(4,1)S(1)}, s32[]{:S(2)}) async-start(s8[6291456]{0:T(1024)(128)(4,1)} %bitcast.4), calls=%async_computation.1 | async-start | bytes 4194304

commit v3 on v2

--- a/solution.py
+++ b/solution.py
@@ -90,7 +90,6 @@
     rho_ref, picked_ref, weight_ref, partial_ref, own_ref, high_ref, low_ref, x_ref, first_inv, second_inv, mid_ref
 ):
     blocks, windows, slots, members = picked_ref.shape
-    half = members // 2
     slot_eye = (
         lax.broadcasted_iota(jnp.int32, (slots, slots), 0)
         == lax.broadcasted_iota(jnp.int32, (slots, slots), 1)
@@ -161,9 +160,7 @@
         w = windows - 2 - turn
         partial_ref[w] = dot_three(partial_ref[w + 1], partial_ref[w])
 
-    own_ref[0] = partial_ref[0, :half, :half].astype(BF16)
-    own_ref[1] = partial_ref[0, half:, :half].astype(BF16)
-    own_ref[2] = partial_ref[0, half:, half:].astype(BF16)
+    own_ref[...] = partial_ref[0].astype(BF16)
 
 
 def direct(high_ref, low_ref, gram, x_ref, first_inv, second_inv, mid_ref):
@@ -194,66 +191,120 @@
         x_ref[w, half:, half:] = second_inv[w]
 
 
-def exchange_kernel(axis, count, one_way, items, *refs):
-    ins, outs = refs[:items], refs[items : 2 * items]
-    send_sem, recv_sem = refs[2 * items :]
+def suffix_kernel(
+    axis, count, own_ref, later_ref, other, mine, wholes, pair_sem, send_sem, recv_sem, pass_send, pass_recv
+):
+    members = own_ref.shape[0]
+    half = members // 2
+    chips = count // 2
     me = lax.axis_index(axis)
+    chip, core = lax.div(me, 2), lax.rem(me, 2)
+    partner = me + 1 - 2 * core
+    nn = ((1,), (0,))
+    left, right = pl.ds(0, half), pl.ds(half, half)
+    split = half + half // 2
+    pieces = (
+        (pl.ds(0, split), left),
+        (pl.ds(split, members - split), left),
+        (right, right),
+    )
+    owned = ((0,), (1, 2))
+
+    for shift in range(1, chips):
+        wholes[shift, :half, half:] = jnp.zeros((half, half), BF16)
     barrier = pltpu.get_barrier_semaphore()
-    for shift in range(1, count):
+
+    def greet(device):
         pl.semaphore_signal(
-            barrier,
-            inc=1,
-            device_id={axis: lax.rem(me + shift, count)},
+            barrier, inc=1, device_id={axis: device}, device_id_type=pl.DeviceIdType.MESH
+        )
+
+    greet(partner)
+    for shift in range(1, chips):
+        greet(lax.rem(me + 2 * shift, count))
+    pl.semaphore_wait(barrier, chips)
+
+    def copy_to(device, source, target, send, recv):
+        return pltpu.make_async_remote_copy(
+            src_ref=source,
+            dst_ref=target,
+            send_sem=send,
+            recv_sem=recv,
+            device_id={axis: device},
             device_id_type=pl.DeviceIdType.MESH,
         )
-    pl.semaphore_wait(barrier, count - 1)
-
-    def copy_of(shift, item):
-        return pltpu.make_async_remote_copy(
-            src_ref=ins[item],
-            dst_ref=outs[item].at[me],
-            send_sem=send_sem.at[item, shift],
-            recv_sem=recv_sem.at[item, shift],
-            device_id={axis: lax.rem(me + count - shift, count)},
-            device_id_type=pl.DeviceIdType.MESH,
-        )
-
-    def when(condition, action):
-        if one_way:
-            pl.when(condition)(action)
-        else:
-            action()
-
-    order = [(shift, item) for shift in range(1, count) for item in range(items)]
-    for shift, item in order:
-        when(me >= shift, lambda: copy_of(shift, item).start())
-    if not one_way:
-        for item in range(items):
-            outs[item][me] = ins[item][...]
-    for shift, item in order:
-        when(me >= shift, lambda: copy_of(shift, item).wait_send())
-        when(me + shift < count, lambda: copy_of(shift, item).wait_recv())
-
-
-def exchange(axis, one_way, collective_id, *values):
-    count = lax.axis_size(axis)
-    items = len(values)
-    vmem = pl.BlockSpec(memory_space=pltpu.VMEM)
-    return pl.pallas_call(
-        lambda *refs: exchange_kernel(axis, count, one_way, items, *refs),
-        out_shape=tuple(jax.ShapeDtypeStruct((count,) + v.shape, v.dtype) for v in values),
-        in_specs=[vmem] * items,
-        out_specs=(vmem,) * items,
-        scratch_shapes=[
-            pltpu.SemaphoreType.DMA((items, count)),
-            pltpu.SemaphoreType.DMA((items, count)),
-        ],
-        compiler_params=pltpu.CompilerParams(
-            collective_id=collective_id, has_side_effects=True, vmem_limit_bytes=8 * MIB
-        ),
-        cost_estimate=pl.CostEstimate(flops=2 * 10**9, bytes_accessed=MIB, transcendentals=0),
-        name="exchange_" + axis,
-    )(*values)
+
+    def down(shift, p):
+        rows, cols = pieces[p]
+        return copy_to(
+            lax.rem(me + count - 2 * shift, count),
+            mine.at[rows, cols],
+            wholes.at[shift, rows, cols],
+            send_sem.at[shift, p],
+            recv_sem.at[shift, p],
+        )
+
+    def across(shift, p):
+        rows, cols = pieces[p]
+        place = wholes.at[shift, rows, cols]
+        return copy_to(partner, place, place, pass_send.at[shift, p], pass_recv.at[shift, p])
+
+    pair = copy_to(partner, own_ref, other, pair_sem.at[0], pair_sem.at[1])
+    pair.start()
+    pair.wait()
+    first = core == 0
+    low_rows, high_rows = own_ref[...], other[...]
+    later_left = jnp.where(first, high_rows, low_rows)
+    later_right = jnp.where(first, low_rows, high_rows)
+    mine[...] = dot_any(later_left, later_right, nn).astype(BF16)
+
+    for k in range(2):
+        for shift in range(chips - 1, 0, -1):
+
+            @pl.when((core == k) & (chip >= shift))
+            def _():
+                for p in owned[k]:
+                    down(shift, p).start()
+
+    for k in range(2):
+        for shift in range(1, chips):
+
+            @pl.when((core == k) & (chip + shift < chips))
+            def _():
+                for p in owned[k]:
+                    down(shift, p).wait_recv()
+                    across(shift, p).start()
+
+    row = lax.broadcasted_iota(jnp.int32, (members, members), 0)
+    col = lax.broadcasted_iota(jnp.int32, (members, members), 1)
+    later_ref[...] = jnp.where(first, high_rows.astype(F32), jnp.where(row == col, 1.0, 0.0))
+    for shift in range(1, chips):
+
+        @pl.when(chip + shift < chips)
+        def _():
+            for k in range(2):
+
+                @pl.when(core == k)
+                def _():
+                    for p in owned[1 - k]:
+                        across(shift, p).wait_recv()
+
+            high, low = halves(later_ref[...])
+            whole = wholes[shift]
+            later_ref[...] = dot_any(whole, high, nn) + dot_any(whole, low, nn)
+
+    for k in range(2):
+        for shift in range(1, chips):
+
+            @pl.when((core == k) & (chip >= shift))
+            def _():
+                for p in owned[k]:
+                    down(shift, p).wait_send()
+
+            @pl.when((core == k) & (chip + shift < chips))
+            def _():
+                for p in owned[k]:
+                    across(shift, p).wait_send()
 
 
 def observe_kernel(axis, count, chunk, field_ref, cells_hbm, counts_hbm, precision_hbm,
@@ -344,28 +395,10 @@
             rows_copy(shift, w).wait()
 
 
-def apply_kernel(position_ref, field_ref, products_ref, partial_ref, out_ref, whole, later, stage, sems):
-    count = products_ref.shape[0]
-    windows, height, members = field_ref.shape
-    half = members // 2
+def apply_kernel(field_ref, later_ref, partial_ref, out_ref, stage, sems):
+    windows, height, _ = field_ref.shape
     tile = stage.shape[2]
     tiles = height // tile
-    nn = ((1,), (0,))
-    whole[...] = jnp.zeros_like(whole)
-    later[...] = (
-        lax.broadcasted_iota(jnp.int32, (members, members), 0)
-        == lax.broadcasted_iota(jnp.int32, (members, members), 1)
-    ).astype(F32)
-
-    @pl.loop(0, count - 1 - position_ref[0])
-    def _(turn):
-        source = count - 1 - turn
-        whole[:half, :half] = products_ref[source, 0]
-        whole[half:, :half] = products_ref[source, 1]
-        whole[half:, half:] = products_ref[source, 2]
-        high, low = halves(later[...])
-        right = whole[...]
-        later[...] = dot_any(high, right, nn) + dot_any(low, right, nn)
 
     def out_of(w, t):
         return pltpu.make_async_copy(
@@ -373,7 +406,7 @@
         )
 
     for w in range(windows):
-        weight = dot_three(later[...], partial_ref[w]).astype(BF16)
+        weight = dot_three(later_ref[...], partial_ref[w]).astype(BF16)
         for t in range(tiles):
             stage[w, t] = dot_any(
                 field_ref[w, pl.ds(t * tile, tile), :], weight, ((1,), (1,))
@@ -426,7 +459,7 @@
         transforms_kernel,
         out_shape=(
             jax.ShapeDtypeStruct((windows, members, members), F32),
-            jax.ShapeDtypeStruct((3, half, half), BF16),
+            jax.ShapeDtypeStruct((members, members), BF16),
         ),
         in_specs=[smem, vmem, vmem],
         out_specs=(vmem, vmem),
@@ -437,23 +470,40 @@
         cost_estimate=pl.CostEstimate(flops=4 * 10**9, bytes_accessed=2 * MIB, transcendentals=0),
         name="transforms",
     )(inflation, gathered, gathered_weights)
-    (products,) = exchange("tm", True, 1, own)
+    devices = lax.axis_size("tm")
+    hops = pltpu.SemaphoreType.DMA((devices // 2, 3))
+    later = pl.pallas_call(
+        lambda *refs: suffix_kernel("tm", devices, *refs),
+        out_shape=jax.ShapeDtypeStruct((members, members), F32),
+        in_specs=[vmem],
+        out_specs=vmem,
+        scratch_shapes=[
+            pltpu.VMEM((members, members), BF16),
+            pltpu.VMEM((members, members), BF16),
+            pltpu.VMEM((devices // 2, members, members), BF16),
+            pltpu.SemaphoreType.DMA((2,)),
+        ]
+        + [hops] * 4,
+        compiler_params=pltpu.CompilerParams(
+            collective_id=1, has_side_effects=True, vmem_limit_bytes=8 * MIB
+        ),
+        cost_estimate=pl.CostEstimate(flops=2 * 10**9, bytes_accessed=MIB, transcendentals=0),
+        name="suffix",
+    )(own)
     flat = anomalies.reshape(windows, fields * cell_width, members)
     tile = min(512, cell_width)
     result = pl.pallas_call(
         apply_kernel,
         out_shape=jax.ShapeDtypeStruct(flat.shape, BF16),
-        in_specs=[smem, vmem, vmem, vmem],
+        in_specs=[vmem, vmem, vmem],
         out_specs=hbm,
         scratch_shapes=[
-            pltpu.VMEM((members, members), BF16),
-            pltpu.VMEM((members, members), F32),
             pltpu.VMEM((windows, fields * cell_width // tile, tile, members), BF16),
             pltpu.SemaphoreType.DMA((windows, fields * cell_width // tile)),
         ],
         compiler_params=pltpu.CompilerParams(vmem_limit_bytes=16 * MIB),
         name="apply",
-    )(lax.axis_index("tm").astype(jnp.int32)[None], flat, products, partial)
+    )(flat, later, partial)
     return result.reshape(anomalies.shape)
 
 

time: 57.8 us -> 52.7 us (0.912)
  Pallas kernels: 57.4 us -> 52.3 us
    pallas_call x1, Pallas kernels: 12.6 us -> 9.28 us  [local(): pl.pallas_call(lambda *refs: suffix_kernel('tm', devices, *refs), out_sha...]
    pallas_call x1, Pallas kernels: 5.72 us -> 3.97 us  [local(): pl.pallas_call(apply_kernel, out_shape=jax.ShapeDtypeStruct(flat.shape, B...]
where the time goes in v3:
time: 52.7 us; the launch traced here: 52.5 us
  Pallas kernels  52.3 us (99%)
    pallas_call x1, Pallas kernels, local(): pl.pallas_call(transforms_kernel, out_shape=(jax.ShapeDtypeStruct((window...  27.5 us
    pallas_call x1, Pallas kernels, local(): pl.pallas_call(lambda *refs: observe_kernel('cell', count, chunk, *refs),...  11.5 us
    pallas_call x1, Pallas kernels, local(): pl.pallas_call(lambda *refs: suffix_kernel('tm', devices, *refs), out_sha...  9.28 us
    pallas_call x1, Pallas kernels, local(): pl.pallas_call(apply_kernel, out_shape=jax.ShapeDtypeStruct(flat.shape, B...  3.97 us

profile of v3, /device:TPU:0, one launch (start us, length us, event | category | flops | bytes accessed | tf_op | source)
XLA Modules:
  0.0 52.5 jit_solution(14583443102388532372)
XLA Ops:
  0.0 0.0 copy-start
  0.0 11.5 %observe.1 = (bf16[4,3,32,256]{3,2,1,0:T(8,128)(2,1)S(1)}, f32[4,3,32]{2,1,0:T(4,128)S(1)}) custom-call(bf16[3,2,2048,256]{3,2,1,0:T(8,128)(2,1)} %refs_0_.1, s32[3,32]{1,0:T(4,128)} %refs_1_.1, s32[3]{0:T(128)} %bitcast.6, f32[3,32]{1,0:T(4,128)} %refs_3_.1), custom_call_target="tpu_custom_call" | custom-call | flops 2000000000 | bytes 1048576 | tf_op jit(solution)/shard_map/observe/pallas_call | solution.py:429
  11.5 0.0 slice-start
  11.5 0.0 copy-done
  11.6 0.0 slice-start.1
  11.6 27.5 %transforms.1 = (f32[3,256,256]{2,1,0:T(8,128)S(1)}, bf16[256,256]{1,0:T(8,128)(2,1)S(1)}) custom-call(f32[3]{0:T(128)S(1)} %copy-done, bf16[4,3,32,256]{3,2,1,0:T(8,128)(2,1)S(1)} %get-tuple-element.9.picked_ref, f32[4,3,32]{2,1,0:T(4,128)S(1)} %get-tuple-element.10.weight_ref), custom_call_target="tpu_custom_call" | custom-call | flops 4000000000 | bytes 2097152 | tf_op jit(solution)/shard_map/transforms/pallas_call | solution.py:458
  39.1 9.3 %suffix.1.later_ref = f32[256,256]{1,0:T(8,128)S(1)} custom-call(bf16[256,256]{1,0:T(8,128)(2,1)S(1)} %get-tuple-element.11.refs_0_), custom_call_target="tpu_custom_call" | custom-call | flops 2000000000 | bytes 1048576 | tf_op jit(solution)/shard_map/suffix/pallas_call | solution.py:475
  48.4 0.0 slice-done
  48.4 0.0 slice-done.1
  48.4 4.0 %apply.1 = bf16[3,4096,256]{2,1,0:T(8,128)(2,1)} custom-call(bf16[3,4096,256]{2,1,0:T(8,128)(2,1)S(1)} %bitcast.5, f32[256,256]{1,0:T(8,128)S(1)} %suffix.1.later_ref, f32[3,256,256]{2,1,0:T(8,128)S(1)} %get-tuple-element.12.partial_ref), custom_call_target="tpu_custom_call" | custom-call | tf_op jit(solution)/shard_map/apply/pallas_call | solution.py:495
  (1 shorter events, 0.0 us)
Async XLA Ops:
  0.0 11.5 %copy-start = (f32[3]{0:T(128)S(1)}, f32[3]{0:T(128)}, u32[]{:S(2)}) copy-start(f32[3]{0:T(128)} %rho_ref.1) | copy-start | bytes 40
  11.5 36.8 %slice-start = ((s8[6291456]{0:T(1024)(128)(4,1)}), s8[4194304]{0:T(1024)(128)(4,1)S(1)}, s32[]{:S(2)}) async-start(s8[6291456]{0:T(1024)(128)(4,1)} %bitcast.3), calls=%async_computation | async-start | bytes 8388608
  11.6 36.8 %slice-start.1 = ((s8[6291456]{0:T(1024)(128)(4,1)}), s8[2097152]{0:T(1024)(128)(4,1)S(1)}, s32[]{:S(2)}) async-start(s8[6291456]{0:T(1024)(128)(4,1)} %bitcast.3), calls=%async_computation.1 | async-start | bytes 4194304

commit v4 on v3

--- a/solution.py
+++ b/solution.py
@@ -8,7 +8,7 @@
 F32 = jnp.float32
 BF16 = jnp.bfloat16
 SPREAD_GAIN = 1.4
-SETTLED = 4e-4
+SETTLED = 2e-3
 MIB = 1 << 20
 
 
@@ -101,45 +101,84 @@
     tn = ((0,), (0,))
     nt = ((1,), (1,))
 
-    for w in range(windows):
-        rows = jnp.concatenate([picked_ref[n, w] for n in range(blocks)], axis=0)
-        columns = [
-            jnp.sum(jnp.where(slot_eye, weight_ref[n, w : w + 1, :], 0.0), axis=1, keepdims=True)
-            for n in range(blocks)
-        ]
-        high, low = halves(rows.astype(F32) * jnp.concatenate(columns, axis=0))
-        system = dot_any(high, rows, tn) + dot_any(low, rows, tn) + jnp.where(eye, F32(members - 1.0), 0.0)
-        high_ref[w], low_ref[w] = halves(system)
-        diagonal = jnp.where(eye, system, 0.0)
-        scale_row = lax.rsqrt(jnp.sum(diagonal, axis=0, keepdims=True))
-        scale_col = lax.rsqrt(jnp.sum(diagonal, axis=1, keepdims=True))
-        corr = system * scale_col * scale_row
-        off = jnp.where(eye, 0.0, corr)
-        spread = jnp.sum(jnp.sum(off * off, axis=0, keepdims=True), axis=1, keepdims=True)
-        beta = 1.0 / (1.0 + SPREAD_GAIN * jnp.sqrt(spread * (1.0 / members)))
-        change = lower_half(beta * corr - jnp.where(eye, 1.0, 0.0), row, col)
-        narrow = change.astype(BF16)
-        second = dot_any(narrow, narrow, nn) + lower_half(dot_any(narrow, narrow, nt), row, col)
-        unit = jnp.where(eye, 1.0, 0.0) - change + second
-        x_ref[w] = unit * (scale_row * jnp.sqrt(beta))
+    unit = jnp.where(eye, 1.0, 0.0)
+
+    every = range(windows)
+
+    def squares(changes):
+        narrow = [change.astype(BF16) for change in changes]
+        plain = [dot_any(n, n, nn) for n in narrow]
+        crossed = [dot_any(n, n, nt) for n in narrow]
+        return [p + lower_half(c, row, col) for p, c in zip(plain, crossed)]
+
+    def correct(narrow_x, changes):
+        steps = [(c - s).astype(BF16) for c, s in zip(changes, squares(changes))]
+        moves = [dot_any(step, narrow_x[w], nn) for w, step in enumerate(steps)]
+        for w in every:
+            x_ref[w] -= moves[w]
+
+    rows = [jnp.concatenate([picked_ref[n, w] for n in range(blocks)], axis=0) for w in every]
+    columns = [
+        jnp.concatenate(
+            [
+                jnp.sum(
+                    jnp.where(slot_eye, weight_ref[n, w : w + 1, :], 0.0), axis=1, keepdims=True
+                )
+                for n in range(blocks)
+            ],
+            axis=0,
+        )
+        for w in every
+    ]
+    wide = [value.astype(F32) for value in rows]
+    scaled = [wide[w] * columns[w] for w in every]
+    scale_rows = [
+        jnp.sqrt(1.0 / (jnp.sum(scaled[w] * wide[w], axis=0, keepdims=True) + F32(members - 1.0)))
+        for w in every
+    ]
+    near_rows = [(wide[w] * (jnp.sqrt(columns[w]) * scale_rows[w])).astype(BF16) for w in every]
+    offs = [jnp.where(eye, 0.0, dot_any(value, value, tn)) for value in near_rows]
+    splits = [halves(value) for value in scaled]
+    for w in every:
+        system = dot_any(rows[w], splits[w][0], tn) + dot_any(rows[w], splits[w][1], tn)
+        high_ref[w], low_ref[w] = halves(system + F32(members - 1.0) * unit)
+    spreads = [
+        jnp.sum(jnp.sum(off * off, axis=0, keepdims=True), axis=1, keepdims=True) for off in offs
+    ]
+    betas = [1.0 / (1.0 + SPREAD_GAIN * jnp.sqrt(spread * (1.0 / members))) for spread in spreads]
+    changes = [
+        jnp.where(row > col, beta * off, jnp.where(eye, 0.5 * (beta - 1.0), 0.0))
+        for beta, off in zip(betas, offs)
+    ]
+    scales = [scale_rows[w] * jnp.sqrt(betas[w]) for w in every]
+
+    for w, second in enumerate(squares(changes)):
+        x_ref[w] = (unit - changes[w] + second) * scales[w]
+
+    xh = [x_ref[w].astype(BF16) for w in every]
+    left = [dot_any(xh[w], high_ref[w], nn).astype(BF16) for w in every]
+    correct(xh, [lower_half(dot_any(left[w], xh[w], nt) - unit, row, col) for w in every])
 
     def refine(state):
         turn, _ = state
         worst = jnp.zeros((1, 1), F32)
-        for w in range(windows):
-            x = x_ref[w]
-            xh, xl = halves(x)
-            ah = high_ref[w]
-            left = dot_any(xh, ah, nn) + (dot_any(xh, low_ref[w], nn) + dot_any(xl, ah, nn))
-            lh, ll = halves(left)
-            near = dot_any(lh, xh, nt) + (dot_any(lh, xl, nt) + dot_any(ll, xh, nt))
-            change = lower_half(near - jnp.where(eye, 1.0, 0.0), row, col)
+        xs = [halves(x_ref[w]) for w in every]
+        left = [
+            dot_any(xs[w][0], high_ref[w], nn)
+            + (dot_any(xs[w][0], low_ref[w], nn) + dot_any(xs[w][1], high_ref[w], nn))
+            for w in every
+        ]
+        ls = [halves(value) for value in left]
+        near = [
+            dot_any(ls[w][0], xs[w][0], nt)
+            + (dot_any(ls[w][0], xs[w][1], nt) + dot_any(ls[w][1], xs[w][0], nt))
+            for w in every
+        ]
+        changes = [lower_half(value - unit, row, col) for value in near]
+        for change in changes:
             size = jnp.sum(jnp.sum(change * change, axis=0, keepdims=True), axis=1, keepdims=True)
             worst = jnp.where(size <= worst, worst, size)
-            narrow = change.astype(BF16)
-            square = lower_half(dot_any(narrow, narrow, nt), row, col).astype(BF16)
-            rest = (x - dot_any(narrow, xh, nn)).astype(BF16)
-            x_ref[w] = x - dot_any(narrow, rest, nn) + dot_any(square, xh, nn)
+        correct([x[0] for x in xs], changes)
         return turn + 1, worst[0, 0]
 
     def again(state):
@@ -399,17 +438,26 @@
     windows, height, _ = field_ref.shape
     tile = stage.shape[2]
     tiles = height // tile
+    nn = ((1,), (0,))
 
     def out_of(w, t):
         return pltpu.make_async_copy(
             stage.at[w, t], out_ref.at[w, pl.ds(t * tile, tile), :], sems.at[w, t]
         )
 
-    for w in range(windows):
-        weight = dot_three(later_ref[...], partial_ref[w]).astype(BF16)
+    high, low = halves(later_ref[...])
+    parts = [halves(partial_ref[w]) for w in range(windows)]
+    weights = [
+        (
+            dot_any(high, parts[w][0], nn)
+            + (dot_any(high, parts[w][1], nn) + dot_any(low, parts[w][0], nn))
+        ).astype(BF16)
+        for w in range(windows)
+    ]
+    for w in range(windows):
         for t in range(tiles):
             stage[w, t] = dot_any(
-                field_ref[w, pl.ds(t * tile, tile), :], weight, ((1,), (1,))
+                field_ref[w, pl.ds(t * tile, tile), :], weights[w], ((1,), (1,))
             ).astype(BF16)
             out_of(w, t).start()
     for w in range(windows):

time: 52.7 us -> 51.3 us (0.973)
  Pallas kernels: 52.3 us -> 50.9 us
    pallas_call x1, Pallas kernels: 27.5 us -> 26.5 us  [local(): pl.pallas_call(transforms_kernel, out_shape=(jax.ShapeDtypeStruct((window...]
where the time goes in v4:
time: 51.3 us; the launch traced here: 51.1 us
  Pallas kernels  50.9 us (99%)
    pallas_call x1, Pallas kernels, local(): pl.pallas_call(transforms_kernel, out_shape=(jax.ShapeDtypeStruct((window...  26.5 us
    pallas_call x1, Pallas kernels, local(): pl.pallas_call(lambda *refs: observe_kernel('cell', count, chunk, *refs),...  11.5 us
    pallas_call x1, Pallas kernels, local(): pl.pallas_call(lambda *refs: suffix_kernel('tm', devices, *refs), out_sha...  9.28 us
    pallas_call x1, Pallas kernels, local(): pl.pallas_call(apply_kernel, out_shape=jax.ShapeDtypeStruct(flat.shape, B...  3.54 us

profile of v4, /device:TPU:0, one launch (start us, length us, event | category | flops | bytes accessed | tf_op | source)
XLA Modules:
  0.0 51.1 jit_solution(12258259801781329066)
XLA Ops:
  0.0 0.0 copy-start
  0.0 11.5 %observe.1 = (bf16[4,3,32,256]{3,2,1,0:T(8,128)(2,1)S(1)}, f32[4,3,32]{2,1,0:T(4,128)S(1)}) custom-call(bf16[3,2,2048,256]{3,2,1,0:T(8,128)(2,1)} %refs_0_.1, s32[3,32]{1,0:T(4,128)} %refs_1_.1, s32[3]{0:T(128)} %bitcast.6, f32[3,32]{1,0:T(4,128)} %refs_3_.1), custom_call_target="tpu_custom_call" | custom-call | flops 2000000000 | bytes 1048576 | tf_op jit(solution)/shard_map/observe/pallas_call | solution.py:477
  11.5 0.0 slice-start
  11.5 0.0 copy-done
  11.6 0.0 slice-start.1
  11.6 26.5 %transforms.1 = (f32[3,256,256]{2,1,0:T(8,128)S(1)}, bf16[256,256]{1,0:T(8,128)(2,1)S(1)}) custom-call(f32[3]{0:T(128)S(1)} %copy-done, bf16[4,3,32,256]{3,2,1,0:T(8,128)(2,1)S(1)} %get-tuple-element.9.picked_ref, f32[4,3,32]{2,1,0:T(4,128)S(1)} %get-tuple-element.10.weight_ref), custom_call_target="tpu_custom_call" | custom-call | flops 4000000000 | bytes 2097152 | tf_op jit(solution)/shard_map/transforms/pallas_call | solution.py:506
  38.1 9.3 %suffix.1.later_ref = f32[256,256]{1,0:T(8,128)S(1)} custom-call(bf16[256,256]{1,0:T(8,128)(2,1)S(1)} %get-tuple-element.11.refs_0_), custom_call_target="tpu_custom_call" | custom-call | flops 2000000000 | bytes 1048576 | tf_op jit(solution)/shard_map/suffix/pallas_call | solution.py:523
  47.4 0.0 slice-done
  47.4 0.0 slice-done.1
  47.4 3.5 %apply.1 = bf16[3,4096,256]{2,1,0:T(8,128)(2,1)} custom-call(bf16[3,4096,256]{2,1,0:T(8,128)(2,1)S(1)} %bitcast.5, f32[256,256]{1,0:T(8,128)S(1)} %suffix.1.later_ref, f32[3,256,256]{2,1,0:T(8,128)S(1)} %get-tuple-element.12.partial_ref), custom_call_target="tpu_custom_call" | custom-call | tf_op jit(solution)/shard_map/apply/pallas_call | solution.py:543
  (1 shorter events, 0.0 us)
Async XLA Ops:
  0.0 11.5 %copy-start = (f32[3]{0:T(128)S(1)}, f32[3]{0:T(128)}, u32[]{:S(2)}) copy-start(f32[3]{0:T(128)} %rho_ref.1) | copy-start | bytes 40
  11.5 35.9 %slice-start = ((s8[6291456]{0:T(1024)(128)(4,1)}), s8[4194304]{0:T(1024)(128)(4,1)S(1)}, s32[]{:S(2)}) async-start(s8[6291456]{0:T(1024)(128)(4,1)} %bitcast.3), calls=%async_computation | async-start | bytes 8388608
  11.6 35.8 %slice-start.1 = ((s8[6291456]{0:T(1024)(128)(4,1)}), s8[2097152]{0:T(1024)(128)(4,1)S(1)}, s32[]{:S(2)}) async-start(s8[6291456]{0:T(1024)(128)(4,1)} %bitcast.3), calls=%async_computation.1 | async-start | bytes 4194304

commit v5 on v4

--- a/solution.py
+++ b/solution.py
@@ -7,8 +7,8 @@
 
 F32 = jnp.float32
 BF16 = jnp.bfloat16
-SPREAD_GAIN = 1.4
-SETTLED = 2e-3
+SPREAD_GAIN = 1.9
+SETTLED = 2.5e-3
 MIB = 1 << 20
 
 
@@ -426,8 +426,9 @@
             pl.semaphore_wait(barrier, count - 1)
             for shift in range(1, count):
                 weights_copy(shift).start()
-        for shift in range(1, count):
-            rows_copy(shift, w).start()
+        for far in range(count - 1, 0, -1):
+            pl.when(me >= far)(rows_copy(far, w).start)
+            pl.when(me + far < count)(rows_copy(count - far, w).start)
     for shift in range(1, count):
         weights_copy(shift).wait()
         for w in range(windows):

time: 51.3 us -> 51.1 us (level)
  no operation moved by 1% of the time
where the time goes in v5:
time: 51.1 us; the launch traced here: 51 us
  Pallas kernels  50.7 us (99%)
    pallas_call x1, Pallas kernels, local(): pl.pallas_call(transforms_kernel, out_shape=(jax.ShapeDtypeStruct((window...  26.5 us
    pallas_call x1, Pallas kernels, local(): pl.pallas_call(lambda *refs: observe_kernel('cell', count, chunk, *refs),...  11.3 us
    pallas_call x1, Pallas kernels, local(): pl.pallas_call(lambda *refs: suffix_kernel('tm', devices, *refs), out_sha...  9.28 us
    pallas_call x1, Pallas kernels, local(): pl.pallas_call(apply_kernel, out_shape=jax.ShapeDtypeStruct(flat.shape, B...  3.54 us

profile of v5, /device:TPU:0, one launch (start us, length us, event | category | flops | bytes accessed | tf_op | source)
XLA Modules:
  0.0 51.0 jit_solution(8579517875537363052)
XLA Ops:
  0.0 0.0 copy-start
  0.0 11.3 %observe.1 = (bf16[4,3,32,256]{3,2,1,0:T(8,128)(2,1)S(1)}, f32[4,3,32]{2,1,0:T(4,128)S(1)}) custom-call(bf16[3,2,2048,256]{3,2,1,0:T(8,128)(2,1)} %refs_0_.1, s32[3,32]{1,0:T(4,128)} %refs_1_.1, s32[3]{0:T(128)} %bitcast.6, f32[3,32]{1,0:T(4,128)} %refs_3_.1), custom_call_target="tpu_custom_call" | custom-call | flops 2000000000 | bytes 1048576 | tf_op jit(solution)/shard_map/observe/pallas_call | solution.py:478
  11.4 0.0 slice-start
  11.4 0.0 copy-done
  11.4 0.0 slice-start.1
  11.4 26.5 %transforms.1 = (f32[3,256,256]{2,1,0:T(8,128)S(1)}, bf16[256,256]{1,0:T(8,128)(2,1)S(1)}) custom-call(f32[3]{0:T(128)S(1)} %copy-done, bf16[4,3,32,256]{3,2,1,0:T(8,128)(2,1)S(1)} %get-tuple-element.9.picked_ref, f32[4,3,32]{2,1,0:T(4,128)S(1)} %get-tuple-element.10.weight_ref), custom_call_target="tpu_custom_call" | custom-call | flops 4000000000 | bytes 2097152 | tf_op jit(solution)/shard_map/transforms/pallas_call | solution.py:507
  37.9 9.3 %suffix.1.later_ref = f32[256,256]{1,0:T(8,128)S(1)} custom-call(bf16[256,256]{1,0:T(8,128)(2,1)S(1)} %get-tuple-element.11.refs_0_), custom_call_target="tpu_custom_call" | custom-call | flops 2000000000 | bytes 1048576 | tf_op jit(solution)/shard_map/suffix/pallas_call | solution.py:524
  47.2 0.0 slice-done
  47.2 0.0 slice-done.1
  47.2 3.5 %apply.1 = bf16[3,4096,256]{2,1,0:T(8,128)(2,1)} custom-call(bf16[3,4096,256]{2,1,0:T(8,128)(2,1)S(1)} %bitcast.5, f32[256,256]{1,0:T(8,128)S(1)} %suffix.1.later_ref, f32[3,256,256]{2,1,0:T(8,128)S(1)} %get-tuple-element.12.partial_ref), custom_call_target="tpu_custom_call" | custom-call | tf_op jit(solution)/shard_map/apply/pallas_call | solution.py:544
  (1 shorter events, 0.0 us)
Async XLA Ops:
  0.0 11.4 %copy-start = (f32[3]{0:T(128)S(1)}, f32[3]{0:T(128)}, u32[]{:S(2)}) copy-start(f32[3]{0:T(128)} %rho_ref.1) | copy-start | bytes 40
  11.4 35.9 %slice-start = ((s8[6291456]{0:T(1024)(128)(4,1)}), s8[4194304]{0:T(1024)(128)(4,1)S(1)}, s32[]{:S(2)}) async-start(s8[6291456]{0:T(1024)(128)(4,1)} %bitcast.3), calls=%async_computation | async-start | bytes 8388608
  11.4 35.8 %slice-start.1 = ((s8[6291456]{0:T(1024)(128)(4,1)}), s8[2097152]{0:T(1024)(128)(4,1)S(1)}, s32[]{:S(2)}) async-start(s8[6291456]{0:T(1024)(128)(4,1)} %bitcast.3), calls=%async_computation.1 | async-start | bytes 4194304

commit v6 on v5

--- a/solution.py
+++ b/solution.py
@@ -231,7 +231,7 @@
 
 
 def suffix_kernel(
-    axis, count, own_ref, later_ref, other, mine, wholes, pair_sem, send_sem, recv_sem, pass_send, pass_recv
+    axis, count, own_ref, partial_ref, weights_ref, values, other, mine, wholes, pair_sem, send_sem, recv_sem, pass_send, pass_recv
 ):
     members = own_ref.shape[0]
     half = members // 2
@@ -305,6 +305,21 @@
                 for p in owned[k]:
                     down(shift, p).start()
 
+    every = range(partial_ref.shape[0])
+
+    def multiplied(whole, source):
+        split = [halves(source[w]) for w in every]
+        for w, (high, low) in enumerate(split):
+            values[w] = dot_any(whole, high, nn) + dot_any(whole, low, nn)
+
+    @pl.when(first)
+    def _():
+        multiplied(other[...], partial_ref)
+
+    @pl.when(core == 1)
+    def _():
+        values[...] = partial_ref[...]
+
     for k in range(2):
         for shift in range(1, chips):
 
@@ -314,9 +329,6 @@
                     down(shift, p).wait_recv()
                     across(shift, p).start()
 
-    row = lax.broadcasted_iota(jnp.int32, (members, members), 0)
-    col = lax.broadcasted_iota(jnp.int32, (members, members), 1)
-    later_ref[...] = jnp.where(first, high_rows.astype(F32), jnp.where(row == col, 1.0, 0.0))
     for shift in range(1, chips):
 
         @pl.when(chip + shift < chips)
@@ -328,9 +340,9 @@
                     for p in owned[1 - k]:
                         across(shift, p).wait_recv()
 
-            high, low = halves(later_ref[...])
-            whole = wholes[shift]
-            later_ref[...] = dot_any(whole, high, nn) + dot_any(whole, low, nn)
+            multiplied(wholes[shift], values)
+
+    weights_ref[...] = values[...].astype(BF16)
 
     for k in range(2):
         for shift in range(1, chips):
@@ -435,30 +447,21 @@
             rows_copy(shift, w).wait()
 
 
-def apply_kernel(field_ref, later_ref, partial_ref, out_ref, stage, sems):
+def apply_kernel(field_ref, weights_ref, out_ref, stage, sems):
     windows, height, _ = field_ref.shape
     tile = stage.shape[2]
     tiles = height // tile
-    nn = ((1,), (0,))
 
     def out_of(w, t):
         return pltpu.make_async_copy(
             stage.at[w, t], out_ref.at[w, pl.ds(t * tile, tile), :], sems.at[w, t]
         )
 
-    high, low = halves(later_ref[...])
-    parts = [halves(partial_ref[w]) for w in range(windows)]
-    weights = [
-        (
-            dot_any(high, parts[w][0], nn)
-            + (dot_any(high, parts[w][1], nn) + dot_any(low, parts[w][0], nn))
-        ).astype(BF16)
-        for w in range(windows)
-    ]
-    for w in range(windows):
+    for w in range(windows):
+        weight = weights_ref[w]
         for t in range(tiles):
             stage[w, t] = dot_any(
-                field_ref[w, pl.ds(t * tile, tile), :], weights[w], ((1,), (1,))
+                field_ref[w, pl.ds(t * tile, tile), :], weight, ((1,), (1,))
             ).astype(BF16)
             out_of(w, t).start()
     for w in range(windows):
@@ -521,12 +524,13 @@
     )(inflation, gathered, gathered_weights)
     devices = lax.axis_size("tm")
     hops = pltpu.SemaphoreType.DMA((devices // 2, 3))
-    later = pl.pallas_call(
+    weight_mats = pl.pallas_call(
         lambda *refs: suffix_kernel("tm", devices, *refs),
-        out_shape=jax.ShapeDtypeStruct((members, members), F32),
-        in_specs=[vmem],
+        out_shape=jax.ShapeDtypeStruct((windows, members, members), BF16),
+        in_specs=[vmem, vmem],
         out_specs=vmem,
         scratch_shapes=[
+            pltpu.VMEM((windows, members, members), F32),
             pltpu.VMEM((members, members), BF16),
             pltpu.VMEM((members, members), BF16),
             pltpu.VMEM((devices // 2, members, members), BF16),
@@ -538,13 +542,13 @@
         ),
         cost_estimate=pl.CostEstimate(flops=2 * 10**9, bytes_accessed=MIB, transcendentals=0),
         name="suffix",
-    )(own)
+    )(own, partial)
     flat = anomalies.reshape(windows, fields * cell_width, members)
     tile = min(512, cell_width)
     result = pl.pallas_call(
         apply_kernel,
         out_shape=jax.ShapeDtypeStruct(flat.shape, BF16),
-        in_specs=[vmem, vmem, vmem],
+        in_specs=[vmem, vmem],
         out_specs=hbm,
         scratch_shapes=[
             pltpu.VMEM((windows, fields * cell_width // tile, tile, members), BF16),
@@ -552,7 +556,7 @@
         ],
         compiler_params=pltpu.CompilerParams(vmem_limit_bytes=16 * MIB),
         name="apply",
-    )(flat, later, partial)
+    )(flat, weight_mats)
     return result.reshape(anomalies.shape)
 
 

time: 51.1 us -> 51.1 us (level)
    pallas_call x1, Pallas kernels: 9.28 us -> 29.3 us  [local(): pl.pallas_call(lambda *refs: suffix_kernel('tm', devices, *refs), out_sha...]
    pallas_call x1, Pallas kernels: 26.5 us -> 6.8 us  [local(): pl.pallas_call(transforms_kernel, out_shape=(jax.ShapeDtypeStruct((window...]
where the time goes in v6:
time: 51.1 us; the launch traced here: 50.9 us
  Pallas kernels  50.7 us (99%)
    pallas_call x1, Pallas kernels, local(): pl.pallas_call(lambda *refs: suffix_kernel('tm', devices, *refs), out_sha...  29.3 us
    pallas_call x1, Pallas kernels, local(): pl.pallas_call(lambda *refs: observe_kernel('cell', count, chunk, *refs),...  11.3 us
    pallas_call x1, Pallas kernels, local(): pl.pallas_call(transforms_kernel, out_shape=(jax.ShapeDtypeStruct((window...  6.8 us
    pallas_call x1, Pallas kernels, local(): pl.pallas_call(apply_kernel, out_shape=jax.ShapeDtypeStruct(flat.shape, B...  3.18 us

profile of v6, /device:TPU:0, one launch (start us, length us, event | category | flops | bytes accessed | tf_op | source)
XLA Modules:
  0.0 50.9 jit_solution(3800427654799138759)
XLA Ops:
  0.0 0.0 copy-start
  0.0 11.3 %observe.1 = (bf16[4,3,32,256]{3,2,1,0:T(8,128)(2,1)S(1)}, f32[4,3,32]{2,1,0:T(4,128)S(1)}) custom-call(bf16[3,2,2048,256]{3,2,1,0:T(8,128)(2,1)} %refs_0_.1, s32[3,32]{1,0:T(4,128)} %refs_1_.1, s32[3]{0:T(128)} %bitcast.6, f32[3,32]{1,0:T(4,128)} %refs_3_.1), custom_call_target="tpu_custom_call" | custom-call | flops 2000000000 | bytes 1048576 | tf_op jit(solution)/shard_map/observe/pallas_call | solution.py:481
  11.4 0.0 slice-start
  11.4 0.0 copy-done
  11.4 0.0 slice-start.1
  11.4 6.8 %transforms.1 = (f32[3,256,256]{2,1,0:T(8,128)S(1)}, bf16[256,256]{1,0:T(8,128)(2,1)S(1)}) custom-call(f32[3]{0:T(128)S(1)} %copy-done, bf16[4,3,32,256]{3,2,1,0:T(8,128)(2,1)S(1)} %get-tuple-element.9.picked_ref, f32[4,3,32]{2,1,0:T(4,128)S(1)} %get-tuple-element.10.weight_ref), custom_call_target="tpu_custom_call" | custom-call | flops 4000000000 | bytes 2097152 | tf_op jit(solution)/shard_map/transforms/pallas_call | solution.py:510
  18.2 29.3 %suffix.1.weights_ref = bf16[3,256,256]{2,1,0:T(8,128)(2,1)S(1)} custom-call(bf16[256,256]{1,0:T(8,128)(2,1)S(1)} %get-tuple-element.11.refs_0_, f32[3,256,256]{2,1,0:T(8,128)S(1)} %get-tuple-element.12.refs_1_), custom_call_target="tpu_custom_call" | custom-call | flops 2000000000 | bytes 1048576 | tf_op jit(solution)/shard_map/suffix/pallas_call | solution.py:527
  47.5 0.0 slice-done
  47.5 0.0 slice-done.1
  47.6 3.2 %apply.1 = bf16[3,4096,256]{2,1,0:T(8,128)(2,1)} custom-call(bf16[3,4096,256]{2,1,0:T(8,128)(2,1)S(1)} %bitcast.5, bf16[3,256,256]{2,1,0:T(8,128)(2,1)S(1)} %suffix.1.weights_ref), custom_call_target="tpu_custom_call" | custom-call | tf_op jit(solution)/shard_map/apply/pallas_call | solution.py:548
  (1 shorter events, 0.0 us)
Async XLA Ops:
  0.0 11.4 %copy-start = (f32[3]{0:T(128)S(1)}, f32[3]{0:T(128)}, u32[]{:S(2)}) copy-start(f32[3]{0:T(128)} %rho_ref.1) | copy-start | bytes 40
  11.4 36.2 %slice-start = ((s8[6291456]{0:T(1024)(128)(4,1)}), s8[4194304]{0:T(1024)(128)(4,1)S(1)}, s32[]{:S(2)}) async-start(s8[6291456]{0:T(1024)(128)(4,1)} %bitcast.3), calls=%async_computation | async-start | bytes 8388608
  11.4 36.2 %slice-start.1 = ((s8[6291456]{0:T(1024)(128)(4,1)}), s8[2097152]{0:T(1024)(128)(4,1)S(1)}, s32[]{:S(2)}) async-start(s8[6291456]{0:T(1024)(128)(4,1)} %bitcast.3), calls=%async_computation.1 | async-start | bytes 4194304
